TPU v7x, 32 devices: a whole 2x2x4 slice. The times are simulated.
32 devices in a mesh: freq: 2 (over x), panel: 16 (over z, y, core).
Axes of the slice: x: 2, y: 2, z: 4, core: 2. Of those that a mesh axis runs over, the one named last changes fastest.
Arguments:
- recorded: float32 [2, 2, 2048, 2048], P('freq', None, 'panel'), parts along dimension 0, may hold values from -60 to 60
- receiver_kernel: bfloat16 [2, 2, 4095], P('freq'), parts along dimension 0, may hold values from -1.5 to 1.5
- source_kernel: bfloat16 [2, 2, 4095], P('freq'), parts along dimension 0, may hold values from -1.5 to 1.5
Outputs:
- primaries: float32 [2, 2, 2048, 2048], P('freq', None, 'panel'), parts along dimension 0
- multiples: bfloat16 [2, 2, 2048, 2048], P('freq', None, 'panel'), parts along dimension 0
There are 2 independent parts, one for each index of `freq`. A program takes and returns all parts, laid end to end along the dimension named above; each array names one. Nothing has to cross between parts.
All inputs are finite; a program needn't handle non-finite values.
Results may differ from a plain program's by a relative error of at most 0.0057.
Values may be sent and summed in bfloat16 or wider, within the bound.
A program may use at most 320 MiB of HBM per device.

v0:
```python
import jax
import jax.numpy as jnp
from jax import lax
from jax.sharding import PartitionSpec as P


def band(kernel, base, nrows, ncols):
    length = nrows + ncols - 1
    piece = lax.dynamic_slice_in_dim(kernel, base - nrows + 1, length, 1)
    rolled = jnp.roll(piece, -(nrows - 1), axis=1)
    flat = jnp.tile(rolled, (1, nrows))[:, : nrows * (length - 1)]
    return flat.reshape(2, nrows, length - 1)[:, :, :ncols]


def complex_dot(left, right):
    real_part = jnp.dot(left[0], right[0], preferred_element_type=jnp.float32) - jnp.dot(
        left[1], right[1], preferred_element_type=jnp.float32
    )
    imag_part = jnp.dot(left[0], right[1], preferred_element_type=jnp.float32) + jnp.dot(
        left[1], right[0], preferred_element_type=jnp.float32
    )
    return jnp.stack([real_part, imag_part])


def per_device(recorded, receiver_kernel, source_kernel):
    freqs, rows, width = (recorded.shape[0], recorded.shape[2], recorded.shape[3])
    panels = lax.axis_size("panel")
    sources = rows * panels
    data_b = recorded.astype(jnp.bfloat16)
    focused = jnp.stack(
        [complex_dot(data_b[0], band(receiver_kernel[0], width - 1, width, width))]
    ).astype(jnp.bfloat16)
    row_first = lax.axis_index("panel") * rows
    local_oper = jnp.stack([band(source_kernel[0], sources - 1 - row_first, rows, sources)])
    oper = local_oper[0]
    parts = [complex_dot(oper, lax.all_gather(focused, "panel", axis=2, tiled=True)[0])]
    summed = jnp.stack(parts)
    mult = summed.astype(jnp.bfloat16)
    mfl = mult.astype(jnp.float32)
    num_re = jnp.sum(mfl[:, 0] * recorded[:, 0] + mfl[:, 1] * recorded[:, 1], axis=(1, 2))
    num_im = jnp.sum(mfl[:, 0] * recorded[:, 1] - mfl[:, 1] * recorded[:, 0], axis=(1, 2))
    energy = jnp.sum(mfl[:, 0] * mfl[:, 0] + mfl[:, 1] * mfl[:, 1], axis=(1, 2))
    num_re, num_im, energy = lax.psum((num_re, num_im, energy), "panel")
    den = energy + 1e-06
    fit_re = (num_re / den)[:, None, None]
    fit_im = (num_im / den)[:, None, None]
    prim_re = recorded[:, 0] - (fit_re * mfl[:, 0] - fit_im * mfl[:, 1])
    prim_im = recorded[:, 1] - (fit_re * mfl[:, 1] + fit_im * mfl[:, 0])
    return (jnp.stack([prim_re, prim_im], axis=1), mult)


def solution(mesh):
    placed = (P("freq", None, "panel", None), P("freq", None, None), P("freq", None, None))
    return jax.shard_map(
        per_device,
        mesh=mesh,
        in_specs=placed,
        out_specs=(P("freq", None, "panel", None), P("freq", None, "panel", None)),
        check_vma=False,
    )
```

profile of v0, /device:TPU:0, one launch (start us, length us, event | category | flops | bytes accessed | tf_op | source)
XLA Modules:
  0.0 487.0 jit_solution(3146243379102983382)
XLA Ops:
  7.2 0.0 copy-start
  7.2 0.0 all-gather.2.cloned.1.call-start
  7.2 0.8 slice.112
  8.0 0.7 slice.113
  8.7 11.0 %tile.20 = bf16[2,2048,4095]{2,1,0:T(8,128)(2,1)} broadcast(bf16[2,4095]{1,0:T(2,128)(2,1)S(1)} %pad_maximum_fusion.3), dimensions={0,2} | broadcast | bytes 33562620 | tf_op jit(solution)/shard_map/tile | solution.py:11
  19.7 69.5 %reshape.271 = bf16[16773120]{0:T(1024)(128)(2,1)} reshape(bf16[2,2048,4095]{2,1,0:T(8,128)(2,1)} %tile.20) | data formatting | bytes 67092480
  89.2 39.9 %tile.21 = bf16[2,8386560]{1,0:T(2,128)(2,1)} reshape(bf16[16773120]{0:T(1024)(128)(2,1)} %reshape.271) | data formatting | bytes 67092480 | tf_op jit(solution)/shard_map/tile | solution.py:11
  129.2 27.0 %slice.114 = bf16[2,8384512]{1,0:T(2,128)(2,1)} slice(bf16[2,8386560]{1,0:T(2,128)(2,1)} %tile.21), slice={[0:2], [0:8384512]} | slice | bytes 67076096 | tf_op jit(solution)/shard_map/slice | solution.py:11
  156.2 52.8 %reshape.273 = bf16[16769024]{0:T(1024)(128)(2,1)} reshape(bf16[2,8384512]{1,0:T(2,128)(2,1)} %slice.114) | data formatting | bytes 67076096
  209.0 0.0 copy-start.1
  209.0 53.4 %reshape.270 = bf16[2,2048,4094]{2,1,0:T(8,128)(2,1)} reshape(bf16[16769024]{0:T(1024)(128)(2,1)} %reshape.273) | data formatting | bytes 67076096 | tf_op jit(solution)/shard_map/reshape | solution.py:12
  262.3 0.0 copy-done.1
  262.4 0.1 convert_element_type.36
  262.5 5.8 %fusion.1 = f32[2048,128]{1,0:T(8,128)S(1)} fusion(bf16[2,2048,4094]{2,1,0:T(8,128)(2,1)} %reshape.270, bf16[1,2,128,2048]{3,2,1,0:T(8,128)(2,1)S(1)} %convert_element_type.36), kind=kOutput, calls=%fused_computation.5 | convolution fusion | flops 1073741824 | bytes 9961472 | tf_op jit(solution)/shard_map/dot_general | solution.py:16
  268.3 5.8 %fusion = f32[2048,128]{1,0:T(8,128)S(1)} fusion(bf16[2,2048,4094]{2,1,0:T(8,128)(2,1)} %reshape.270, bf16[1,2,128,2048]{3,2,1,0:T(8,128)(2,1)S(1)} %convert_element_type.36), kind=kOutput, calls=%fused_computation.4 | convolution fusion | flops 1073741824 | bytes 9961472 | tf_op jit(solution)/shard_map/dot_general | solution.py:19
  274.2 5.8 %fusion.18 = bf16[1,1,128,2048]{2,3,1,0:T(8,128)(2,1)S(1)} fusion(f32[2048,128]{1,0:T(8,128)S(1)} %fusion.1, bf16[2,2048,4094]{2,1,0:T(8,128)(2,1)} %reshape.270, bf16[1,2,128,2048]{3,2,1,0:T(8,128)(2,1)S(1)} %convert_element_type.36), kind=kOutput, calls=%fused_computation.22 | convolution fusion | flops 1074266112 | bytes 10485760 | tf_op jit(solution)/shard_map/dot_general | solution.py:16
  280.0 5.8 %fusion.19 = bf16[1,1,128,2048]{2,3,1,0:T(8,128)(2,1)S(1)} fusion(f32[2048,128]{1,0:T(8,128)S(1)} %fusion, bf16[2,2048,4094]{2,1,0:T(8,128)(2,1)} %reshape.270, bf16[1,2,128,2048]{3,2,1,0:T(8,128)(2,1)S(1)} %convert_element_type.36), kind=kOutput, calls=%fused_computation.23 | convolution fusion | flops 1074266112 | bytes 10485760 | tf_op jit(solution)/shard_map/dot_general | solution.py:19
  285.8 1.1 pad_maximum_fusion.1
  286.9 0.0 all-gather.2.cloned.1.call-update
  286.9 0.0 copy-done
  286.9 0.1 dynamic-slice_bitcast_fusion
  287.0 0.1 slice.108
  287.1 0.1 tile.8
  287.2 2.5 reshape.275
  289.7 3.0 tile.9
  292.7 2.0 slice.110
  294.7 3.1 reshape.277
  297.8 3.0 reshape.269
  300.8 0.0 copy-start.3
  300.8 118.8 %all-gather.2.cloned.1.call-done = bf16[1,2,2048,2048]{2,3,1,0:T(8,128)(2,1)} async-done(((bf16[1,2,128,2048]{2,3,1,0:T(8,128)(2,1)}), bf16[1,2,2048,2048]{2,3,1,0:T(8,128)(2,1)}) %all-gather.2.cloned.1.call-update) | async-done | bytes 16777232 | tf_op jit(solution)/shard_map/all_gather | solution.py:36
  419.7 0.0 copy-start.4
  419.7 6.6 %fusion.5 = f32[128,2048]{1,0:T(8,128)S(1)} fusion(bf16[1,2,2048,2048]{2,3,1,0:T(8,128)(2,1)} %all-gather.2.cloned.1.call-done, bf16[2,128,2174]{2,1,0:T(8,128)(2,1)} %reshape.269), kind=kOutput, calls=%fused_computation.9 | convolution fusion | flops 1073741824 | bytes 9961472 | tf_op jit(solution)/shard_map/dot_general | solution.py:16
  426.2 0.0 copy-done.3
  426.3 7.0 %fusion.4 = f32[128,2048]{1,0:T(8,128)S(1)} fusion(bf16[1,2,2048,2048]{2,3,1,0:T(8,128)(2,1)} %all-gather.2.cloned.1.call-done, bf16[2,128,2174]{2,1,0:T(8,128)(2,1)S(1)} %copy-done.3), kind=kOutput, calls=%fused_computation.8 | convolution fusion | flops 1073741824 | bytes 9961472 | tf_op jit(solution)/shard_map/dot_general | solution.py:19
  433.3 0.0 copy-done.4
  433.3 2.9 fusion.16
  436.2 2.9 fusion.17
  439.1 1.2 fusion.20
  440.3 0.0 copy-start.2
  440.3 1.3 copy-done.2
  441.6 1.6 add_reduce_fusion.1
  443.2 31.4 %all-reduce = (f32[1]{0:T(128)}, f32[1]{0:T(128)}, f32[1]{0:T(128)}) all-reduce(f32[1]{0:T(128)} %bitcast.19, f32[1]{0:T(128)} %bitcast.17, f32[1]{0:T(128)} %bitcast.16), channel_id=1, replica_groups=mesh['freq'=2,'panel'=16] {'panel'}, use_global_device_ids=true, to_apply=%region_5.6 | all-reduce | flops 3 | bytes 24 | tf_op jit(solution)/shard_map/psum | solution.py:43
  476.4 1.9 subtract_subtract_fusion
  478.3 1.5 pad_maximum_fusion
  (3 shorter events, 0.0 us)
Async XLA Ops:
  7.2 279.7 %copy-start = (bf16[1,2,4095]{2,1,0:T(2,128)(2,1)S(1)}, bf16[1,2,4095]{2,1,0:T(2,128)(2,1)}, u32[]{:S(2)}) copy-start(bf16[1,2,4095]{2,1,0:T(2,128)(2,1)} %param.5) | copy-start | bytes 49144
  7.2 412.5 %all-gather.2.cloned.1.call-start = ((), (), s32[]{:S(2)}) async-start(), calls=%async_computation | async-start | bytes 17825792 | tf_op jit(solution)/shard_map/all_gather | solution.py:36
  209.0 53.4 %copy-start.1 = (f32[1,2,128,2048]{3,2,1,0:T(8,128)S(1)}, f32[1,2,128,2048]{3,2,1,0:T(8,128)}, u32[]{:S(2)}) copy-start(f32[1,2,128,2048]{3,2,1,0:T(8,128)} %param.3) | copy-start | bytes 6291460
  300.8 125.4 %copy-start.3 = (bf16[2,128,2174]{2,1,0:T(8,128)(2,1)S(1)}, bf16[2,128,2174]{2,1,0:T(8,128)(2,1)}, u32[]{:S(2)}) copy-start(bf16[2,128,2174]{2,1,0:T(8,128)(2,1)} %reshape.269) | copy-start | bytes 3339268
  419.7 13.6 %copy-start.4 = (bf16[1,2,2048,2048]{2,3,1,0:T(8,128)(2,1)S(1)}, bf16[1,2,2048,2048]{2,3,1,0:T(8,128)(2,1)}, u32[]{:S(2)}) copy-start(bf16[1,2,2048,2048]{2,3,1,0:T(8,128)(2,1)} %all-gather.2.cloned.1.call-done) | copy-start | bytes 50331652
  440.3 1.3 copy-start.2
Sparse Core Ops, SparseCore 0:
  287.0 132.6 all-gather.1
where the time goes:
time: 496 us; the launch traced here: 487 us
  local copies, waits for them, and re-layouts  270 us (54%)
  waiting for transfers between devices  119 us (24%)
  matrix products  42.7 us (9%)
  blocking collectives  31.4 us (6%)
  between operations  16.4 us (3%)
  other arithmetic  7.4 us (1%)
    unnamed x14, local copies, waits for them, and re-layouts  129 us
    all_gather x1, waiting for transfers between devices, per_device(): lax.all_gather(focused, 'panel', axis=2, tiled=True)[0]  119 us
    reshape x2, local copies, waits for them, and re-layouts, band(): return flat.reshape(2, nrows, length - 1)[:, :, :ncols]  56.4 us
    another operation x4, local copies, waits for them, and re-layouts, band(): flat = jnp.tile(rolled, (1, nrows))[:, :nrows * (length - 1)]  54 us
    psum x1, blocking collectives, per_device(): num_re, num_im, energy = lax.psum((num_re, num_im, energy), 'panel')  31.4 us
    slice x2, local copies, waits for them, and re-layouts, band(): flat = jnp.tile(rolled, (1, nrows))[:, :nrows * (length - 1)]  29 us
    dot_general x2, matrix products, complex_dot(): jnp.dot(left[1], right[0], preferred_element_type=jnp.float32)  12.8 us
    dot_general x2, matrix products, complex_dot(): jnp.dot(left[0], right[0], preferred_element_type=jnp.float32)  12.4 us
  transfers between devices with their start and end apart: 1, of which 1 were waited for; matrix products, arithmetic and copies ran while one was open for 3% of the time, Pallas kernels for 0%

commit v1 on v0

v1 whole, which is shorter than its diff:
```python
import functools

import jax
import jax.numpy as jnp
from jax import lax
from jax.experimental import pallas as pl
from jax.experimental.pallas import tpu as pltpu
from jax.sharding import PartitionSpec as P

MESH = pl.DeviceIdType.MESH
LANES = 128
GROUP = 256
STRIP = 16


def skew(taps_ref, comp, block, lane0, band_ref):
    length = taps_ref.shape[1]
    x = jnp.broadcast_to(taps_ref[comp : comp + 1, :], (STRIP, length))
    row = lax.broadcasted_iota(jnp.int32, (STRIP, length), 0)
    step = 1
    while step < STRIP:
        x = jnp.where((row & step) != 0, pltpu.roll(x, step, 1), x)
        step *= 2
    for s in range(0, LANES, STRIP):
        shift = (s - (LANES - block)) % length
        y = (pltpu.roll(x, shift, 1) if shift else x).astype(jnp.bfloat16)
        for m in range(length // LANES):
            at = length - LANES * (m + 1)
            band_ref[m * LANES + s : m * LANES + s + STRIP, lane0 : lane0 + block] = y[:, at : at + block]


def exchange_kernel(
    panels,
    rec_ref,
    rtaps_ref,
    staps_ref,
    mult_ref,
    fit_ref,
    band_r,
    band_s,
    w1,
    w2,
    foc,
    foc_in,
    mul,
    mul_in,
    sums,
    sums_in,
    send1,
    recv1,
    send2,
    recv2,
    send3,
    recv3,
):
    me = lax.axis_index("panel")
    rows, width = rec_ref.shape[2], rec_ref.shape[3]
    sources = rows * panels
    cols = width // panels
    nt = (((1,), (1,)), ((), ()))

    def peer(o):
        return lax.rem(me + o, panels)

    barrier = pltpu.get_barrier_semaphore()

    @pl.loop(1, panels)
    def _(o):
        pl.semaphore_signal(barrier, inc=1, device_id={"panel": peer(o)}, device_id_type=MESH)

    for kb in range(width // LANES):
        re = rec_ref[0, 0, :, kb * LANES : (kb + 1) * LANES].astype(jnp.bfloat16)
        im = rec_ref[0, 1, :, kb * LANES : (kb + 1) * LANES].astype(jnp.bfloat16)
        at = 2 * kb * LANES
        w1[0:rows, at : at + LANES] = re
        w1[0:rows, at + LANES : at + 2 * LANES] = -im
        w1[rows : 2 * rows, at : at + LANES] = im
        w1[rows : 2 * rows, at + LANES : at + 2 * LANES] = re
    skew(rtaps_ref, 0, LANES, 0, band_r)
    skew(rtaps_ref, 1, LANES, LANES, band_r)

    pl.semaphore_wait(barrier, panels - 1)

    def copy1(dest, src):
        return pltpu.make_async_remote_copy(
            src_ref=foc.at[pl.ds(pl.multiple_of(dest * cols, cols), cols), :],
            dst_ref=foc_in.at[src],
            send_sem=send1.at[dest],
            recv_sem=recv1.at[src],
            device_id={"panel": dest},
            device_id_type=MESH,
        )

    def copy2(dest, src):
        return pltpu.make_async_remote_copy(
            src_ref=mul.at[pl.ds(pl.multiple_of(dest * rows, rows), rows), :],
            dst_ref=mul_in.at[src],
            send_sem=send2.at[dest],
            recv_sem=recv2.at[src],
            device_id={"panel": dest},
            device_id_type=MESH,
        )

    def copy3(dest, src):
        return pltpu.make_async_remote_copy(
            src_ref=sums,
            dst_ref=sums_in.at[src],
            send_sem=send3.at[dest],
            recv_sem=recv3.at[src],
            device_id={"panel": dest},
            device_id_type=MESH,
        )

    groups1 = width // GROUP
    per1 = GROUP // cols
    own1 = me // per1

    @pl.loop(0, groups1)
    def _(n):
        g = lax.rem(own1 + 1 + n, groups1)
        first = pl.multiple_of(g * GROUP, GROUP)
        lhs = jnp.concatenate(
            [
                band_r[pl.ds(pl.multiple_of(width - LANES * (kb + 1) + first, LANES), GROUP), :]
                for kb in range(width // LANES)
            ],
            axis=1,
        )
        out = lax.dot_general(lhs, w1[...], nt, preferred_element_type=jnp.float32)
        foc[pl.ds(first, GROUP), :] = out.astype(jnp.bfloat16)
        for d in range(per1):
            dest = g * per1 + d

            @pl.when(dest != me)
            def _():
                copy1(dest, me).start()

    foc_in[me] = foc[pl.ds(pl.multiple_of(me * cols, cols), cols), :]
    skew(staps_ref, 0, rows, 0, band_s)
    skew(staps_ref, 1, rows, rows, band_s)

    @pl.loop(1, panels)
    def _(o):
        copy1(peer(o), peer(o)).wait_recv()

    lane = lax.broadcasted_iota(jnp.int32, (cols, 2 * rows), 1)
    for j in range(panels):
        x = foc_in[j]
        at = 2 * rows * j
        w2[0:cols, at : at + 2 * rows] = jnp.where(lane < rows, x, -x)
        w2[cols : 2 * cols, at : at + 2 * rows] = jnp.concatenate([x[:, rows:], x[:, :rows]], axis=1)

    groups2 = sources // GROUP
    per2 = GROUP // rows
    own2 = me // per2

    @pl.loop(0, groups2)
    def _(n):
        g = lax.rem(own2 + 1 + n, groups2)
        first = pl.multiple_of(g * GROUP, GROUP)
        lhs = jnp.concatenate(
            [
                band_s[pl.ds(pl.multiple_of(sources - rows * (jb + 1) + first, rows), GROUP), :]
                for jb in range(panels)
            ],
            axis=1,
        )
        out = lax.dot_general(lhs, w2[...], nt, preferred_element_type=jnp.float32)
        mul[pl.ds(first, GROUP), :] = out.astype(jnp.bfloat16)
        for d in range(per2):
            dest = g * per2 + d

            @pl.when(dest != me)
            def _():
                copy2(dest, me).start()

    mul_in[me] = mul[pl.ds(pl.multiple_of(me * rows, rows), rows), :]

    @pl.loop(1, panels)
    def _(o):
        copy2(peer(o), peer(o)).wait_recv()

    def fold(v):
        return jnp.sum(v, axis=0, keepdims=True)

    num_re = jnp.zeros((1, LANES), jnp.float32)
    num_im = jnp.zeros((1, LANES), jnp.float32)
    energy = jnp.zeros((1, LANES), jnp.float32)
    per = LANES // cols
    for cb in range(width // LANES):
        blocks = [mul_in[cb * per + d] for d in range(per)]
        mre = jnp.concatenate([b[:, :cols] for b in blocks], axis=1)
        mim = jnp.concatenate([b[:, cols:] for b in blocks], axis=1)
        at = cb * LANES
        mult_ref[0, 0, :, at : at + LANES] = mre
        mult_ref[0, 1, :, at : at + LANES] = mim
        mre = mre.astype(jnp.float32)
        mim = mim.astype(jnp.float32)
        pre = rec_ref[0, 0, :, at : at + LANES]
        pim = rec_ref[0, 1, :, at : at + LANES]
        num_re += fold(mre * pre + mim * pim)
        num_im += fold(mre * pim - mim * pre)
        energy += fold(mre * mre + mim * mim)
    part = jnp.concatenate([num_re, num_im, energy, jnp.zeros((5, LANES), jnp.float32)], axis=0)
    sums[...] = part
    sums_in[me] = part

    @pl.loop(1, panels)
    def _(o):
        copy3(peer(o), me).start()

    @pl.loop(1, panels)
    def _(o):
        copy1(peer(o), me).wait_send()
        copy2(peer(o), me).wait_send()

    @pl.loop(1, panels)
    def _(o):
        copy3(peer(o), peer(o)).wait_recv()

    @pl.loop(1, panels)
    def _(o):
        copy3(peer(o), me).wait_send()

    total = jnp.sum(jnp.sum(sums_in[...], axis=0), axis=1, keepdims=True)
    fit = total[0:2, :] / (total[2:3, :] + 1e-06)
    fit_ref[...] = jnp.broadcast_to(
        jnp.concatenate([fit, jnp.zeros((6, 1), jnp.float32)], axis=0), (8, LANES)
    )


def subtract_kernel(rec_ref, mult_in_ref, fit_ref, prim_ref, mult_ref):
    fit_re = fit_ref[0:1, 0:1]
    fit_im = fit_ref[1:2, 0:1]
    mult_ref[...] = mult_in_ref[...]
    mre = mult_in_ref[0, 0].astype(jnp.float32)
    mim = mult_in_ref[0, 1].astype(jnp.float32)
    prim_ref[0, 0] = rec_ref[0, 0] - (fit_re * mre - fit_im * mim)
    prim_ref[0, 1] = rec_ref[0, 1] - (fit_re * mim + fit_im * mre)


def per_device(recorded, receiver_kernel, source_kernel):
    rows, width = recorded.shape[2], recorded.shape[3]
    panels = lax.axis_size("panel")
    sources = rows * panels
    cols = width // panels
    pad = ((0, 0), (1, 0))
    rtaps = jnp.pad(jnp.flip(receiver_kernel[0].astype(jnp.float32), axis=1), pad)
    staps = jnp.pad(source_kernel[0].astype(jnp.float32), pad)
    bf16 = jnp.bfloat16
    vmem = pl.BlockSpec(memory_space=pltpu.VMEM)
    sem = pltpu.SemaphoreType.DMA((panels,))
    mult, fit = pl.pallas_call(
        functools.partial(exchange_kernel, panels),
        out_shape=(
            jax.ShapeDtypeStruct(recorded.shape, bf16),
            jax.ShapeDtypeStruct((8, LANES), jnp.float32),
        ),
        in_specs=[vmem] * 3,
        out_specs=(vmem, vmem),
        scratch_shapes=[
            pltpu.VMEM((2 * width, 2 * LANES), bf16),
            pltpu.VMEM((2 * sources, 2 * rows), bf16),
            pltpu.VMEM((2 * rows, 2 * width), bf16),
            pltpu.VMEM((2 * cols, 2 * sources), bf16),
            pltpu.VMEM((width, 2 * rows), bf16),
            pltpu.VMEM((panels, cols, 2 * rows), bf16),
            pltpu.VMEM((sources, 2 * cols), bf16),
            pltpu.VMEM((panels, rows, 2 * cols), bf16),
            pltpu.VMEM((8, LANES), jnp.float32),
            pltpu.VMEM((panels, 8, LANES), jnp.float32),
            sem,
            sem,
            sem,
            sem,
            sem,
            sem,
        ],
        compiler_params=pltpu.CompilerParams(collective_id=0, has_side_effects=True, vmem_limit_bytes=56 * 2**20),
        name="exchange",
    )(recorded, rtaps, staps)
    strip = rows // 4
    block = pl.BlockSpec((1, 2, strip, width), lambda i: (0, 0, i, 0))
    return pl.pallas_call(
        subtract_kernel,
        grid=(rows // strip,),
        out_shape=(
            jax.ShapeDtypeStruct(recorded.shape, jnp.float32),
            jax.ShapeDtypeStruct(recorded.shape, bf16),
        ),
        in_specs=[block, block, pl.BlockSpec((8, LANES), lambda i: (0, 0))],
        out_specs=(block, block),
        name="subtract",
    )(recorded, mult, fit)


def solution(mesh):
    placed = (P("freq", None, "panel", None), P("freq", None, None), P("freq", None, None))
    return jax.shard_map(
        per_device,
        mesh=mesh,
        in_specs=placed,
        out_specs=(P("freq", None, "panel", None), P("freq", None, "panel", None)),
        check_vma=False,
    )
```

time: 496 us -> 77 us (0.16); the launches traced: 487 us -> 76.6 us
  local copies, waits for them, and re-layouts: 270 us -> 3.62 us
  waiting for transfers between devices: 119 us -> 0 us
  Pallas kernels: 0 us -> 70.2 us
  matrix products: 42.7 us -> 0 us
  blocking collectives: 31.4 us -> 0 us
  between operations: 16.4 us -> 0.65 us
  other arithmetic: 7.4 us -> 2.15 us
    unnamed x14 -> x2, local copies, waits for them, and re-layouts: 129 us -> 2.89 us
    all_gather x1 -> x0, waiting for transfers between devices: 119 us -> none  [per_device(): lax.all_gather(focused, 'panel', axis=2, tiled=True)[0]]
    pallas_call x0 -> x2, Pallas kernels: none -> 70.2 us  [the longest x1 65.8 us: per_device(): pl.pallas_call(functools.partial(exchange_kernel, panels), out_shape=(jax...]
    reshape x2 -> x0, local copies, waits for them, and re-layouts: 56.4 us -> none  [band(): return flat.reshape(2, nrows, length - 1)[:, :, :ncols]]
    another operation x4 -> x0, local copies, waits for them, and re-layouts: 54 us -> none  [band(): flat = jnp.tile(rolled, (1, nrows))[:, :nrows * (length - 1)]]
    dot_general x8 -> x0, matrix products: 42.7 us -> none  [the longest x2 12.8 us: complex_dot(): jnp.dot(left[1], right[0], preferred_element_type=jnp.float32)]
    psum x1 -> x0, blocking collectives: 31.4 us -> none  [per_device(): num_re, num_im, energy = lax.psum((num_re, num_im, energy), 'panel')]
    slice x6 -> x0, local copies, waits for them, and re-layouts: 30.6 us -> none  [the longest x2 29 us: band(): flat = jnp.tile(rolled, (1, nrows))[:, :nrows * (length - 1)]]
  transfers between devices with their start and end apart: 1 -> 0, of which waited for: 1 -> 0; matrix products, arithmetic and copies ran while one was open for 3% -> 0% of each run, Pallas kernels for 0% -> 0%
where the time goes in v1:
time: 77 us; the launch traced here: 76.6 us
  Pallas kernels  70.2 us (91%)
  local copies, waits for them, and re-layouts  3.62 us (5%)
  other arithmetic  2.15 us (3%)
    pallas_call x1, Pallas kernels, per_device(): pl.pallas_call(functools.partial(exchange_kernel, panels), out_shape=(jax...  65.8 us
    pallas_call x1, Pallas kernels, per_device(): pl.pallas_call(subtract_kernel, grid=(rows // strip,), out_shape=(jax.Sha...  4.43 us
    unnamed x2, local copies, waits for them, and re-layouts  2.89 us

profile of v1, /device:TPU:0, one launch (start us, length us, event | category | flops | bytes accessed | tf_op | source)
XLA Modules:
  0.0 76.6 jit_solution(11152782773940748801)
XLA Ops:
  0.6 0.7 bitcast_convert_fusion
  1.4 2.8 %reverse = f32[2,4096]{1,0:T(2,128)S(1)} reverse(f32[2,4096]{1,0:T(2,128)S(1)} %bitcast.5), dimensions={1} | reverse | bytes 65536
  4.2 0.1 slice
  4.3 0.7 pad.9.rtaps_ref
  5.0 1.4 %pad_convert_fusion.staps_ref = f32[2,4096]{1,0:T(2,128)} fusion(bf16[2,4095]{1,0:T(2,128)(2,1)} %bitcast.6), kind=kLoop, calls=%fused_computation.1 | loop fusion | flops 8192 | bytes 49148 | tf_op jit(solution)/shard_map/jit(_pad)/pad | solution.py:249
  6.4 65.8 %exchange.1 = (bf16[1,2,128,2048]{3,2,1,0:T(8,128)(2,1)}, f32[8,128]{1,0:T(8,128)}) custom-call(f32[1,2,128,2048]{3,2,1,0:T(8,128)} %rec_ref.3, f32[2,4096]{1,0:T(2,128)} %pad.9.rtaps_ref, f32[2,4096]{1,0:T(2,128)} %pad_convert_fusion.staps_ref), custom_call_target="tpu_custom_call" | custom-call | tf_op jit(solution)/shard_map/exchange/pallas_call | solution.py:253
  72.2 4.4 %subtract.1 = (f32[1,2,128,2048]{3,2,1,0:T(8,128)}, bf16[1,2,128,2048]{3,2,1,0:T(8,128)(2,1)}) custom-call(f32[1,2,128,2048]{3,2,1,0:T(8,128)} %rec_ref.3, bf16[1,2,128,2048]{3,2,1,0:T(8,128)(2,1)} %get-tuple-element.4.mult_in_ref, f32[8,128]{1,0:T(8,128)} %get-tuple-element.5.fit_ref), custom_call_target="tpu_custom_call" | custom-call | tf_op jit(solution)/shard_map/subtract/pallas_call | solution.py:284

commit v2 on v1

v2 whole, which is shorter than its diff:
```python
import functools

import jax
import jax.numpy as jnp
from jax import lax
from jax.experimental import pallas as pl
from jax.experimental.pallas import tpu as pltpu
from jax.sharding import PartitionSpec as P

MESH = pl.DeviceIdType.MESH
LANES = 128
GROUP = 256
STRIP = 16
STRIPS = 4


def spread(taps_ref, padded, comp, flipped):
    length = padded.shape[1]
    rows = [padded[comp : comp + 1, at : at + LANES] for at in range(0, length, LANES)]
    if not flipped:
        return jnp.broadcast_to(jnp.concatenate(rows, axis=1), (STRIP, length))
    i = lax.broadcasted_iota(jnp.int32, (LANES, LANES), 0)
    j = lax.broadcasted_iota(jnp.int32, (LANES, LANES), 1)
    swap = jnp.where(i + j == LANES - 1, 1.0, 0.0).astype(jnp.bfloat16)
    tall = jnp.concatenate([jnp.broadcast_to(r, (STRIP, LANES)) for r in rows[::-1]], axis=0)
    tall = jnp.dot(tall.astype(jnp.bfloat16), swap, preferred_element_type=jnp.float32)
    return jnp.concatenate([tall[at : at + STRIP] for at in range(0, tall.shape[0], STRIP)], axis=1)


def skew(taps_ref, padded, flipped, block, band_ref):
    length = padded.shape[1]
    padded[...] = jnp.zeros_like(padded)
    padded[:, 0 : length - 1] = taps_ref[0].astype(jnp.float32)
    row = lax.broadcasted_iota(jnp.int32, (STRIP, length), 0)
    for comp in range(2):
        x = spread(taps_ref, padded, comp, flipped)
        step = 1
        while step < STRIP:
            x = jnp.where((row & step) != 0, pltpu.roll(x, step, 1), x)
            step *= 2
        lane0 = comp * block
        for s in range(0, LANES, STRIP):
            shift = (s - (LANES - block) + (0 if flipped else 1)) % length
            y = (pltpu.roll(x, shift, 1) if shift else x).astype(jnp.bfloat16)
            for m in range(length // LANES):
                at = length - LANES * (m + 1)
                band_ref[m * LANES + s : m * LANES + s + STRIP, lane0 : lane0 + block] = y[:, at : at + block]


def exchange_kernel(
    panels,
    rec_hbm,
    rtaps_hbm,
    staps_hbm,
    rec_ref,
    mult_ref,
    fit_ref,
    rtaps_ref,
    staps_ref,
    load_sem,
    padded,
    band_r,
    band_s,
    w1,
    w2,
    foc,
    foc_in,
    mul,
    mul_in,
    sums,
    sums_in,
    send1,
    recv1,
    send2,
    recv2,
    send3,
    recv3,
):
    me = lax.axis_index("panel")
    rows, width = rec_ref.shape[2], rec_ref.shape[3]
    sources = rows * panels
    cols = width // panels
    halves, hc = foc_in.shape[0], foc_in.shape[2]
    nt = (((1,), (1,)), ((), ()))

    def order(n, own, groups):
        side = groups // 2
        half = lax.rem(own // side + 1 + n // side, 2)
        return half * side + lax.rem(own + 1 + n, side)

    def peer(o):
        return lax.rem(me + o, panels)

    loads = [
        pltpu.make_async_copy(src, dst, load_sem.at[i])
        for i, (src, dst) in enumerate(
            ((rtaps_hbm, rtaps_ref), (rec_hbm, rec_ref), (staps_hbm, staps_ref))
        )
    ]
    for load in loads:
        load.start()

    barrier = pltpu.get_barrier_semaphore()

    @pl.loop(1, panels)
    def _(o):
        pl.semaphore_signal(barrier, inc=1, device_id={"panel": peer(o)}, device_id_type=MESH)

    loads[0].wait()
    skew(rtaps_ref, padded, True, LANES, band_r)
    loads[1].wait()
    for kb in range(width // LANES):
        re = rec_ref[0, 0, :, kb * LANES : (kb + 1) * LANES].astype(jnp.bfloat16)
        im = rec_ref[0, 1, :, kb * LANES : (kb + 1) * LANES].astype(jnp.bfloat16)
        at = 2 * kb * LANES
        w1[0:rows, at : at + LANES] = re
        w1[0:rows, at + LANES : at + 2 * LANES] = -im
        w1[rows : 2 * rows, at : at + LANES] = im
        w1[rows : 2 * rows, at + LANES : at + 2 * LANES] = re

    pl.semaphore_wait(barrier, panels - 1)

    def copy1(h, dest, src):
        return pltpu.make_async_remote_copy(
            src_ref=foc.at[pl.ds(pl.multiple_of(dest * cols + h * hc, hc), hc), :],
            dst_ref=foc_in.at[h, src],
            send_sem=send1.at[h, dest],
            recv_sem=recv1.at[h, src],
            device_id={"panel": dest},
            device_id_type=MESH,
        )

    def copy2(h, dest, src):
        return pltpu.make_async_remote_copy(
            src_ref=mul.at[h, pl.ds(pl.multiple_of(dest * rows, rows), rows), :],
            dst_ref=mul_in.at[h, src],
            send_sem=send2.at[h, dest],
            recv_sem=recv2.at[h, src],
            device_id={"panel": dest},
            device_id_type=MESH,
        )

    def copy3(dest, src):
        return pltpu.make_async_remote_copy(
            src_ref=sums,
            dst_ref=sums_in.at[src],
            send_sem=send3.at[dest],
            recv_sem=recv3.at[src],
            device_id={"panel": dest},
            device_id_type=MESH,
        )

    groups1 = width // GROUP
    per1 = GROUP // cols
    own1 = me // per1

    @pl.loop(0, groups1)
    def _(n):
        g = order(n, own1, groups1)
        first = pl.multiple_of(g * GROUP, GROUP)
        lhs = jnp.concatenate(
            [
                band_r[pl.ds(pl.multiple_of(width - LANES * (kb + 1) + first, LANES), GROUP), :]
                for kb in range(width // LANES)
            ],
            axis=1,
        )
        out = lax.dot_general(lhs, w1[...], nt, preferred_element_type=jnp.float32)
        foc[pl.ds(first, GROUP), :] = out.astype(jnp.bfloat16)
        for d in range(per1):
            dest = g * per1 + d

            @pl.when(dest != me)
            def _():
                copy1(0, dest, me).start()

    for h in range(1, halves):

        @pl.loop(0, groups1)
        def _(n):
            for d in range(per1):
                dest = order(n, own1, groups1) * per1 + d

                @pl.when(dest != me)
                def _():
                    copy1(h, dest, me).start()

    for h in range(halves):
        foc_in[h, me] = foc[pl.ds(pl.multiple_of(me * cols + h * hc, hc), hc), :]
    loads[2].wait()
    skew(staps_ref, padded, False, rows, band_s)

    groups2 = sources // GROUP
    per2 = GROUP // rows
    own2 = me // per2
    lane = lax.broadcasted_iota(jnp.int32, (hc, 2 * rows), 1)
    for h in range(halves):

        @pl.loop(1, panels)
        def _(o):
            copy1(h, peer(o), peer(o)).wait_recv()

        for j in range(panels):
            x = foc_in[h, j]
            at = 2 * rows * j
            w2[0:hc, at : at + 2 * rows] = jnp.where(lane < rows, x, -x)
            w2[hc : 2 * hc, at : at + 2 * rows] = jnp.concatenate([x[:, rows:], x[:, :rows]], axis=1)

        @pl.loop(0, groups2)
        def _(n):
            g = order(n, own2, groups2)
            first = pl.multiple_of(g * GROUP, GROUP)
            lhs = jnp.concatenate(
                [
                    band_s[pl.ds(pl.multiple_of(sources - rows * (jb + 1) + first, rows), GROUP), :]
                    for jb in range(panels)
                ],
                axis=1,
            )
            out = lax.dot_general(lhs, w2[...], nt, preferred_element_type=jnp.float32)
            mul[h, pl.ds(first, GROUP), :] = out.astype(jnp.bfloat16)
            for d in range(per2):
                dest = g * per2 + d

                @pl.when(dest != me)
                def _():
                    copy2(h, dest, me).start()

        mul_in[h, me] = mul[h, pl.ds(pl.multiple_of(me * rows, rows), rows), :]

    def fold(v):
        return jnp.sum(v, axis=0, keepdims=True)

    chunks = width // LANES
    near = LANES // cols

    def gather(n, acc):
        cb = order(n, me // near, chunks)
        blocks = []
        for d in range(near):
            src = cb * near + d

            @pl.when(src != me)
            def _():
                for h in range(halves):
                    copy2(h, src, src).wait_recv()

            blocks += [mul_in[h, src] for h in range(halves)]
        mre = jnp.concatenate([b[:, :hc] for b in blocks], axis=1)
        mim = jnp.concatenate([b[:, hc:] for b in blocks], axis=1)
        at = pl.ds(pl.multiple_of(cb * LANES, LANES), LANES)
        mult_ref[0, 0, :, at] = mre
        mult_ref[0, 1, :, at] = mim
        mre = mre.astype(jnp.float32)
        mim = mim.astype(jnp.float32)
        pre = rec_ref[0, 0, :, at]
        pim = rec_ref[0, 1, :, at]
        return (
            acc[0] + fold(mre * pre + mim * pim),
            acc[1] + fold(mre * pim - mim * pre),
            acc[2] + fold(mre * mre + mim * mim),
        )

    zero = jnp.zeros((1, LANES), jnp.float32)
    num_re, num_im, energy = lax.fori_loop(0, chunks, gather, (zero, zero, zero))
    part = jnp.concatenate([num_re, num_im, energy, jnp.zeros((5, LANES), jnp.float32)], axis=0)
    sums[...] = part
    sums_in[me] = part

    @pl.loop(1, panels)
    def _(o):
        copy3(peer(o), me).start()

    @pl.loop(1, panels)
    def _(o):
        for h in range(halves):
            copy1(h, peer(o), me).wait_send()
            copy2(h, peer(o), me).wait_send()

    @pl.loop(1, panels)
    def _(o):
        copy3(peer(o), peer(o)).wait_recv()

    @pl.loop(1, panels)
    def _(o):
        copy3(peer(o), me).wait_send()

    total = jnp.sum(jnp.sum(sums_in[...], axis=0), axis=1, keepdims=True)
    fit = total[0:2, :] / (total[2:3, :] + 1e-06)
    fit_ref[...] = jnp.broadcast_to(
        jnp.concatenate([fit, jnp.zeros((6, 1), jnp.float32)], axis=0), (8, LANES)
    )


def subtract_kernel(rec_ref, mult_ref, fit_ref, prim_hbm, mult_hbm, prim, sem):
    mult_out = pltpu.make_async_copy(mult_ref, mult_hbm, sem.at[0])
    mult_out.start()
    fit_re = fit_ref[0:1, 0:1]
    fit_im = fit_ref[1:2, 0:1]
    rows = rec_ref.shape[2]
    strip = rows // STRIPS
    outs = []
    for i in range(STRIPS):
        at = slice(i * strip, (i + 1) * strip)
        mre = mult_ref[0, 0, at, :].astype(jnp.float32)
        mim = mult_ref[0, 1, at, :].astype(jnp.float32)
        prim[0, 0, at, :] = rec_ref[0, 0, at, :] - (fit_re * mre - fit_im * mim)
        prim[0, 1, at, :] = rec_ref[0, 1, at, :] - (fit_re * mim + fit_im * mre)
        out = pltpu.make_async_copy(prim.at[:, :, at, :], prim_hbm.at[:, :, at, :], sem.at[i + 1])
        out.start()
        outs.append(out)
    for out in outs:
        out.wait()
    mult_out.wait()


def per_device(recorded, receiver_kernel, source_kernel):
    rows, width = recorded.shape[2], recorded.shape[3]
    panels = lax.axis_size("panel")
    sources = rows * panels
    cols = width // panels
    bf16 = jnp.bfloat16
    vmem = pl.BlockSpec(memory_space=pltpu.VMEM)
    hc = min(cols, LANES // 2)
    halves = cols // hc
    sem = pltpu.SemaphoreType.DMA((panels,))
    sems = pltpu.SemaphoreType.DMA((halves, panels))
    hbm = pl.BlockSpec(memory_space=pltpu.HBM)
    rec, mult, fit = pl.pallas_call(
        functools.partial(exchange_kernel, panels),
        out_shape=(
            jax.ShapeDtypeStruct(recorded.shape, jnp.float32),
            jax.ShapeDtypeStruct(recorded.shape, bf16),
            jax.ShapeDtypeStruct((8, LANES), jnp.float32),
        ),
        in_specs=[hbm] * 3,
        out_specs=(vmem, vmem, vmem),
        scratch_shapes=[
            pltpu.VMEM(receiver_kernel.shape, bf16),
            pltpu.VMEM(source_kernel.shape, bf16),
            pltpu.SemaphoreType.DMA((3,)),
            pltpu.VMEM((2, 2 * width), jnp.float32),
            pltpu.VMEM((2 * width, 2 * LANES), bf16),
            pltpu.VMEM((2 * sources, 2 * rows), bf16),
            pltpu.VMEM((2 * rows, 2 * width), bf16),
            pltpu.VMEM((2 * hc, 2 * sources), bf16),
            pltpu.VMEM((width, 2 * rows), bf16),
            pltpu.VMEM((halves, panels, hc, 2 * rows), bf16),
            pltpu.VMEM((halves, sources, 2 * hc), bf16),
            pltpu.VMEM((halves, panels, rows, 2 * hc), bf16),
            pltpu.VMEM((8, LANES), jnp.float32),
            pltpu.VMEM((panels, 8, LANES), jnp.float32),
            sems,
            sems,
            sems,
            sems,
            sem,
            sem,
        ],
        compiler_params=pltpu.CompilerParams(collective_id=0, has_side_effects=True, vmem_limit_bytes=32 * 2**20),
        name="exchange",
    )(recorded, receiver_kernel, source_kernel)
    return pl.pallas_call(
        subtract_kernel,
        out_shape=(
            jax.ShapeDtypeStruct(recorded.shape, jnp.float32),
            jax.ShapeDtypeStruct(recorded.shape, bf16),
        ),
        in_specs=[vmem] * 3,
        out_specs=(hbm, hbm),
        scratch_shapes=[pltpu.VMEM(recorded.shape, jnp.float32), pltpu.SemaphoreType.DMA((STRIPS + 1,))],
        compiler_params=pltpu.CompilerParams(vmem_limit_bytes=12 * 2**20),
        name="subtract",
    )(rec, mult, fit)


def solution(mesh):
    placed = (P("freq", None, "panel", None), P("freq", None, None), P("freq", None, None))
    return jax.shard_map(
        per_device,
        mesh=mesh,
        in_specs=placed,
        out_specs=(P("freq", None, "panel", None), P("freq", None, "panel", None)),
        check_vma=False,
    )
```

time: 77 us -> 65.9 us (0.86)
  Pallas kernels: 70.2 us -> 61.9 us
  other arithmetic: 2.15 us -> 0 us
    pallas_call x1, Pallas kernels: 65.8 us -> 60.2 us  [per_device(): pl.pallas_call(functools.partial(exchange_kernel, panels), out_shape=(jax...]
    pallas_call x1, Pallas kernels: 4.43 us -> 1.7 us  [per_device(): pl.pallas_call(subtract_kernel, out_shape=(jax.ShapeDtypeStruct(recorded....]
    pad x1 -> x0, other arithmetic: 1.42 us -> none  [per_device(): staps = jnp.pad(source_kernel[0].astype(jnp.float32), pad)]
    unnamed x2 -> x6, local copies, waits for them, and re-layouts: 2.89 us -> 3.02 us
where the time goes in v2:
time: 65.9 us; the launch traced here: 65.5 us
  Pallas kernels  61.9 us (94%)
  local copies, waits for them, and re-layouts  3.02 us (5%)
    pallas_call x1, Pallas kernels, per_device(): pl.pallas_call(functools.partial(exchange_kernel, panels), out_shape=(jax...  60.2 us
    unnamed x6, local copies, waits for them, and re-layouts  3.02 us
    pallas_call x1, Pallas kernels, per_device(): pl.pallas_call(subtract_kernel, out_shape=(jax.ShapeDtypeStruct(recorded....  1.7 us

profile of v2, /device:TPU:0, one launch (start us, length us, event | category | flops | bytes accessed | tf_op | source)
XLA Modules:
  0.0 65.5 jit_solution(5835731114885781526)
XLA Ops:
  0.6 0.0 copy-start
  0.6 1.6 %copy-done = f32[1,2,128,2048]{3,2,1,0:T(8,128)S(1)} copy-done((f32[1,2,128,2048]{3,2,1,0:T(8,128)S(1)}, f32[1,2,128,2048]{3,2,1,0:T(8,128)}, u32[]{:S(2)}) %copy-start) | copy-done | bytes 2097176
  2.2 0.0 copy-start.1
  2.2 0.7 %copy-done.1 = bf16[1,2,4095]{2,1,0:T(2,128)(2,1)S(1)} copy-done((bf16[1,2,4095]{2,1,0:T(2,128)(2,1)S(1)}, bf16[1,2,4095]{2,1,0:T(2,128)(2,1)}, u32[]{:S(2)}) %copy-start.1) | copy-done | bytes 16404
  2.9 0.0 copy-start.2
  2.9 0.7 %copy-done.2 = bf16[1,2,4095]{2,1,0:T(2,128)(2,1)S(1)} copy-done((bf16[1,2,4095]{2,1,0:T(2,128)(2,1)S(1)}, bf16[1,2,4095]{2,1,0:T(2,128)(2,1)}, u32[]{:S(2)}) %copy-start.2) | copy-done | bytes 16404
  3.7 60.2 %exchange.1 = (f32[1,2,128,2048]{3,2,1,0:T(8,128)S(1)}, bf16[1,2,128,2048]{3,2,1,0:T(8,128)(2,1)S(1)}, f32[8,128]{1,0:T(8,128)S(1)}) custom-call(f32[1,2,128,2048]{3,2,1,0:T(8,128)S(1)} %copy-done, bf16[1,2,4095]{2,1,0:T(2,128)(2,1)S(1)} %copy-done.1, bf16[1,2,4095]{2,1,0:T(2,128)(2,1)S(1)} %copy-done.2), custom_call_target="tpu_custom_call" | custom-call | tf_op jit(solution)/shard_map/exchange/pallas_call | solution.py:329
  63.8 1.7 %subtract.1 = (f32[1,2,128,2048]{3,2,1,0:T(8,128)}, bf16[1,2,128,2048]{3,2,1,0:T(8,128)(2,1)}) custom-call(f32[1,2,128,2048]{3,2,1,0:T(8,128)S(1)} %get-tuple-element.5.rec_ref, bf16[1,2,128,2048]{3,2,1,0:T(8,128)(2,1)S(1)} %get-tuple-element.6.mult_ref, f32[8,128]{1,0:T(8,128)S(1)} %get-tuple-element.7.fit_ref), custom_call_target="tpu_custom_call" | custom-call | tf_op jit(solution)/shard_map/subtract/pallas_call | solution.py:363
Async XLA Ops:
  0.6 1.6 %copy-start = (f32[1,2,128,2048]{3,2,1,0:T(8,128)S(1)}, f32[1,2,128,2048]{3,2,1,0:T(8,128)}, u32[]{:S(2)}) copy-start(f32[1,2,128,2048]{3,2,1,0:T(8,128)} %rec_hbm.1) | copy-start | bytes 6291460
  2.2 0.7 %copy-start.1 = (bf16[1,2,4095]{2,1,0:T(2,128)(2,1)S(1)}, bf16[1,2,4095]{2,1,0:T(2,128)(2,1)}, u32[]{:S(2)}) copy-start(bf16[1,2,4095]{2,1,0:T(2,128)(2,1)} %rtaps_hbm.1) | copy-start | bytes 49144
  2.9 0.7 %copy-start.2 = (bf16[1,2,4095]{2,1,0:T(2,128)(2,1)S(1)}, bf16[1,2,4095]{2,1,0:T(2,128)(2,1)}, u32[]{:S(2)}) copy-start(bf16[1,2,4095]{2,1,0:T(2,128)(2,1)} %staps_hbm.1) | copy-start | bytes 49144

commit v3 on v2

--- a/solution.py
+++ b/solution.py
@@ -357,9 +357,11 @@
             sem,
             sem,
         ],
-        compiler_params=pltpu.CompilerParams(collective_id=0, has_side_effects=True, vmem_limit_bytes=32 * 2**20),
+        compiler_params=pltpu.CompilerParams(collective_id=0, has_side_effects=True, vmem_limit_bytes=50 * 2**20),
         name="exchange",
-    )(recorded, receiver_kernel, source_kernel)
+    )(
+        *(pltpu.with_memory_space_constraint(x, pltpu.HBM) for x in (recorded, receiver_kernel, source_kernel))
+    )
     return pl.pallas_call(
         subtract_kernel,
         out_shape=(

time: 65.9 us -> 62.6 us (0.950)
  local copies, waits for them, and re-layouts: 3.02 us -> 0 us
    unnamed x6 -> x0, local copies, waits for them, and re-layouts: 3.02 us -> none
where the time goes in v3:
time: 62.6 us; the launch traced here: 62.3 us
  Pallas kernels  61.7 us (99%)
  between operations  0.64 us (1%)
    pallas_call x1, Pallas kernels, per_device(): pl.pallas_call(functools.partial(exchange_kernel, panels), out_shape=(jax...  60 us
    pallas_call x1, Pallas kernels, per_device(): pl.pallas_call(subtract_kernel, out_shape=(jax.ShapeDtypeStruct(recorded....  1.7 us

profile of v3, /device:TPU:0, one launch (start us, length us, event | category | flops | bytes accessed | tf_op | source)
XLA Modules:
  0.0 62.3 jit_solution(2097953449456151773)
XLA Ops:
  0.6 60.0 %exchange.1 = (f32[1,2,128,2048]{3,2,1,0:T(8,128)S(1)}, bf16[1,2,128,2048]{3,2,1,0:T(8,128)(2,1)S(1)}, f32[8,128]{1,0:T(8,128)S(1)}) custom-call(f32[1,2,128,2048]{3,2,1,0:T(8,128)} %rec_hbm.1, bf16[1,2,4095]{2,1,0:T(2,128)(2,1)} %rtaps_hbm.1, bf16[1,2,4095]{2,1,0:T(2,128)(2,1)} %staps_hbm.1), custom_call_target="tpu_custom_call" | custom-call | tf_op jit(solution)/shard_map/exchange/pallas_call | solution.py:329
  60.6 1.7 %subtract.1 = (f32[1,2,128,2048]{3,2,1,0:T(8,128)}, bf16[1,2,128,2048]{3,2,1,0:T(8,128)(2,1)}) custom-call(f32[1,2,128,2048]{3,2,1,0:T(8,128)S(1)} %get-tuple-element.5.rec_ref, bf16[1,2,128,2048]{3,2,1,0:T(8,128)(2,1)S(1)} %get-tuple-element.6.mult_ref, f32[8,128]{1,0:T(8,128)S(1)} %get-tuple-element.7.fit_ref), custom_call_target="tpu_custom_call" | custom-call | tf_op jit(solution)/shard_map/subtract/pallas_call | solution.py:365
